TPU v7x, 128 devices: a whole 4x4x4 slice. The times are simulated.
128 devices in a mesh: node: 16 (over z, y), data: 8 (over x, core).
Axes of the slice: x: 4, y: 4, z: 4, core: 2. Of those that a mesh axis runs over, the one named last changes fastest.
Arguments:
- tokens: bfloat16 [131072, 768], P(('node', 'data'))
- grad_out: bfloat16 [131072, 768], P(('node', 'data'))
- weights: bfloat16 [8, 768, 768], replicated
- a_old: float32 [8, 768, 768], replicated
- s_old: float32 [8, 768, 768], replicated
- a_inv: float32 [8, 768, 768], replicated
- s_inv: float32 [8, 768, 768], replicated
Outputs:
- output 1: float32 [8, 768, 768], replicated
- output 2: float32 [8, 768, 768], replicated
- output 3: float32 [8, 768, 768], replicated
All inputs are finite; a program needn't handle non-finite values.
Results may differ from a plain program's by a relative error of at most 0.00169187.
Values are sent between devices in bfloat16 or wider.
A program may use at most 1 GiB of HBM per device.

v0:
```python
import functools

import jax
import jax.numpy as jnp
from jax import lax
from jax.experimental import pallas as pl
from jax.experimental.pallas import tpu as pltpu
from jax.sharding import PartitionSpec as P

FACTOR_DECAY = 0.8
GELU_SCALE = 0.7978845608028654
GELU_CUBIC = 0.044715
MESH = pl.DeviceIdType.MESH
W = 768
ROUNDS = 8
NX, NR, NG = 3, 3, 4
PERIODS = ROUNDS + 5
DIAG_PERIOD = 7
BATCH = 1024
FWD, BWD = 512, 512
HIDDEN = 8
BF16 = jnp.bfloat16
F32 = jnp.float32
ALL = pl.ds(0, W)
SCALE = 1.0 / 131072.0


def comm_kernel(tok_ref, dout_ref, w_ref, ainv_ref, sinv_ref, packed_ref, upd_ref, dsum_ref,
                X, R, G, D, Y, ACT, WB, INV, UPD, MS, ML,
                rsem, ssem, dsend, drecv, isem, osem, osend, orecv, msend, mrecv, mloc, wsem, tsem):
    node, data = lax.axis_index('node'), lax.axis_index('data')
    core = lax.rem(data, 2)
    coord = [data // 2, lax.rem(node, 4), node // 4]

    def device(axis, delta):
        c = list(coord)
        c[axis] = lax.rem(c[axis] + delta + 4, 4)
        return (c[2] * 4 + c[1], c[0] * 2 + core)

    partner = (node, data + 1 - 2 * core)

    barrier = pltpu.get_barrier_semaphore()
    peers = [partner] + [device(a, d) for a in range(3) for d in (1, 2, 3)]
    for dev in peers:
        pl.semaphore_signal(barrier, inc=1, device_id=dev, device_id_type=MESH)
    pl.semaphore_wait(barrier, len(peers))

    def mo(v, m):
        return pl.multiple_of(v, m)

    def send(src, dst, s, r, dev):
        pltpu.make_async_remote_copy(src_ref=src, dst_ref=dst, send_sem=s, recv_sem=r, device_id=dev, device_id_type=MESH).start()

    def wait(ref, sem):
        pltpu.make_async_copy(ref, ref, sem).wait()

    def is_update(p):
        return (p >= 2) & (p < 6)

    def layer_of(p):
        return 11 - 2 * p - core

    def packed_of(p):
        return 2 * jnp.where(p < 2, p, p - 4) + core

    def place(k, s):
        return coord[(k + s) % 3]

    def region(p, k, s, j, half=None, slots=NX):
        row = mo(lax.rem(p, slots) * W, W) + 256 * k
        if s == 0:
            row = row + 64 * j
            n, col, m = 64, 0, W
        elif s == 1:
            row = row + 64 * place(k, 0) + 16 * j
            n, col, m = 16, 0, W
        else:
            row = row + 64 * place(k, 0) + 16 * place(k, 1) + 8 * (j // 2)
            n, col, m = 8, 384 * lax.rem(j, 2), 384
        if half is not None:
            if s < 2:
                n //= 2
                row = row + half * n
            else:
                col, m = (col, 128) if half == 0 else (col + 128, 256)
        row = mo(row, 8)
        if s < 2:
            return pl.ds(row, n), ALL
        return pl.ds(row, n), pl.ds(mo(col, 128), m)

    def landing(p, k, s, what, side=None, half=None):
        row = mo(lax.rem(p, NR) * W, W) + 256 * k
        if s < 2:
            h = (32, 8)[s]
            if side is None:
                start, n = 2 * what, 2 + 2 * what
            elif what == 0:
                start, n = side, 1
            elif half is None:
                start, n = 2 + 2 * side, 2
            else:
                start, n = 2 + 2 * side + half, 1
            return pl.ds(mo(row + 192 * s + start * h, 8), n * h), ALL
        row = pl.ds(mo(row + 240 + 8 * what, 8), 8)
        if side is None:
            return row, pl.ds(0, 384 * (1 + what))
        if what == 0:
            return row, pl.ds(128 * side, 128 * (side + 1))
        if half is None:
            return row, pl.ds(384 * side, 384)
        return row, pl.ds(384 * side + 128 * half, 128 * (half + 1))

    def neighbours(k, s):
        a = (k + s) % 3
        return place(k, s), device(a, 1), device(a, -1)

    def around(i):
        return lax.rem(i + 1, 4), lax.rem(i + 3, 4), lax.rem(i + 2, 4)

    def rs(p, k, s, w):
        return rsem.at[lax.rem(p, NR), (k * 3 + s) * 4 + w]

    def ss(p, k, s, w):
        return ssem.at[lax.rem(p, NR), (k * 3 + s) * 4 + w]

    def add(dst, src):
        X[dst] = X[dst] + R[src]

    def scatter_a(p, k, s):
        i, plus, minus = neighbours(k, s)
        jp, jm, j2 = around(i)
        fwd, blk, sa = rs(p, k, s, 0), rs(p, k, s, 1), ss(p, k, s, 0)
        send(X.at[region(p, k, s, j2, 0)], R.at[landing(p, k, s, 0, 0)], sa, fwd, minus)
        send(X.at[region(p, k, s, j2, 1)], R.at[landing(p, k, s, 0, 1)], sa, fwd, plus)
        send(X.at[region(p, k, s, jm, 1)], R.at[landing(p, k, s, 1, 0, 1)], sa, blk, minus)
        send(X.at[region(p, k, s, jp, 0)], R.at[landing(p, k, s, 1, 1, 0)], sa, blk, plus)

    def scatter_b(p, k, s):
        i, plus, minus = neighbours(k, s)
        jp, jm, _ = around(i)
        blk, sb = rs(p, k, s, 1), ss(p, k, s, 1)
        wait(R.at[landing(p, k, s, 0)], rs(p, k, s, 0))
        add(region(p, k, s, jm, 0), landing(p, k, s, 0, 0))
        send(X.at[region(p, k, s, jm, 0)], R.at[landing(p, k, s, 1, 0, 0)], sb, blk, minus)
        add(region(p, k, s, jp, 1), landing(p, k, s, 0, 1))
        send(X.at[region(p, k, s, jp, 1)], R.at[landing(p, k, s, 1, 1, 1)], sb, blk, plus)

    def scatter_c(p, k, s):
        i = place(k, s)
        wait(R.at[landing(p, k, s, 1)], rs(p, k, s, 1))
        mine = region(p, k, s, i)
        value = X[mine] + (R[landing(p, k, s, 1, 0)] + R[landing(p, k, s, 1, 1)])
        if s < 2:
            X[mine] = value
        else:
            G[region(p, k, s, i, slots=NG)] = value

    def gather_a(p, k, s):
        i, plus, minus = neighbours(k, s)
        mine = G.at[region(p, k, s, i, slots=NG)]
        send(mine, mine, ss(p, k, s, 2), rs(p, k, s, 2), plus)
        send(mine, mine, ss(p, k, s, 2), rs(p, k, s, 2), minus)

    def gather_b(p, k, s):
        i, plus, minus = neighbours(k, s)
        jp, jm, _ = around(i)
        wait(R.at[landing(p, k, s, 1)], rs(p, k, s, 2))
        from_minus, from_plus = G.at[region(p, k, s, jm, 0, slots=NG)], G.at[region(p, k, s, jp, 1, slots=NG)]
        send(from_minus, from_minus, ss(p, k, s, 3), rs(p, k, s, 3), plus)
        send(from_plus, from_plus, ss(p, k, s, 3), rs(p, k, s, 3), minus)

    def gather_c(p, k, s):
        wait(R.at[landing(p, k, s, 0)], rs(p, k, s, 3))

    def colours(f, p, s):
        for k in range(3):
            f(p, k, s)

    def gslot(p):
        return G.at[pl.ds(mo(lax.rem(p, NG) * W, W), W)]

    def xslot(p):
        return X.at[pl.ds(mo(lax.rem(p, NX) * W, W), W)]

    def unit(ref, index):
        return ref.at[pl.ds(mo(index * W, W), W)]

    def dslot(p):
        return D.at[pl.ds(mo(lax.rem(p, 2) * W, W), W)]

    def produced(p, which):
        return mo((lax.rem(p, 2) * 2 + which) * W, W)

    def step0(p):
        send(Y.at[pl.ds(produced(p, 1 - core), W)], dslot(p), dsend.at[lax.rem(p, 2)], drecv.at[lax.rem(p, 2)], partner)

    def step1(p):
        wait(dslot(p), drecv.at[lax.rem(p, 2)])

        def some(c, carry):
            a = pl.ds(mo(lax.rem(p, NX) * W + c * 64, 64), 64)
            X[a, :] = Y[pl.ds(mo(produced(p, core) + c * 64, 64), 64), :] + D[pl.ds(mo(lax.rem(p, 2) * W + c * 64, 64), 64), :]
            return carry
        lax.fori_loop(0, 12, some, 0)
        colours(scatter_a, p, 0)

    def step2(p):
        colours(scatter_b, p, 0)
        wait(dslot(p), dsend.at[lax.rem(p, 2)])

    def step3(p):
        colours(scatter_c, p, 0)
        colours(scatter_a, p, 1)

    def step4(p):
        colours(scatter_b, p, 1)

    def step5(p):
        colours(scatter_c, p, 1)
        colours(scatter_a, p, 2)

    def step6(p):
        colours(scatter_b, p, 2)

    def step7(p):
        colours(scatter_c, p, 2)
        colours(gather_a, p, 2)

    def sent(p, w):
        for k in range(3):
            for s in range(3):
                wait(R.at[landing(p, k, s, 1)], ss(p, k, s, w))
                wait(R.at[landing(p, k, s, 0)], ss(p, k, s, w + 1))

    def step8(p):
        colours(gather_b, p, 2)
        sent(p, 0)

    def step9(p):
        colours(gather_c, p, 2)
        colours(gather_a, p, 1)

    def inverse(which):
        return INV.at[pl.ds(which * W, W)]

    def load_inverses(p):
        l = layer_of(p)
        pltpu.make_async_copy(ainv_ref.at[l], inverse(0), isem.at[0]).start()
        pltpu.make_async_copy(sinv_ref.at[l], inverse(1), isem.at[1]).start()

    def step10(p):
        colours(gather_b, p, 1)

    def step11(p):
        colours(gather_c, p, 1)
        colours(gather_a, p, 0)

    def step12(p):
        colours(gather_b, p, 0)

    def piece(p, part):
        @pl.when(is_update(p))
        def _():
            rows = 256 * part
            a = INV[pl.ds(rows, 256), :]
            g = G[pl.ds(mo(lax.rem(p, NG) * W, W), W), :]
            left = jnp.dot(a, g, precision=lax.Precision.HIGHEST, preferred_element_type=F32) * SCALE
            b = INV[pl.ds(W, W), :]
            here = pl.ds(rows, 256)
            UPD[here, :] = jnp.dot(left, b, precision=lax.Precision.HIGHEST, preferred_element_type=F32)
            out = upd_ref.at[layer_of(p), pl.ds(rows, 256)]
            pltpu.make_async_copy(UPD.at[here], out, osem.at[lax.rem(p, 2)]).start()
            send(UPD.at[here], out, osend.at[lax.rem(p, 2)], orecv.at[p], partner)

    def step13(p):
        colours(gather_c, p, 0)

        @pl.when(is_update(p))
        def _():
            wait(inverse(0), isem.at[0])
            wait(inverse(1), isem.at[1])

        @pl.when(jnp.logical_not(is_update(p)))
        def _():
            out = packed_ref.at[packed_of(p)]
            pltpu.make_async_copy(gslot(p), out, osem.at[lax.rem(p, 2)]).start()
            send(gslot(p), out, osend.at[lax.rem(p, 2)], orecv.at[p], partner)
        piece(p, 0)

    def step14(p):
        sent(p, 2)
        piece(p, 1)

    def step15(p):
        piece(p, 2)

        @pl.when(is_update(p) & is_update(p + 1))
        def _():
            load_inverses(p + 1)

    def step16(p):
        wait(xslot(p), osem.at[lax.rem(p, 2)])
        wait(xslot(p), osend.at[lax.rem(p, 2)])

    def step17(p):
        wait(xslot(p), orecv.at[p])

    steps = [step0, step1, step2, step3, step4, step5, step6, step7, step8, step9, step10, step11, step12, step13, step14, step15, step16, step17]
    slots = [(0, 6, 9, 12, 3, 15), (7, 10, 4, 1, 16, 13), (8, 5, 11, 2, 14, 17)]

    def ms(n):
        return pl.ds(8 * n, 8)

    def small_send(stage):
        if stage == 0:
            send(MS.at[ms(0)], ML.at[ms(0)], msend.at[0], mrecv.at[0], partner)
        else:
            for d in (1, 2, 3):
                n = 3 * stage - 3 + d
                send(MS.at[ms(stage)], ML.at[ms(n)], msend.at[n], mrecv.at[n], device(stage - 1, d))

    def small_take(stage):
        if stage == 0:
            wait(ML.at[ms(0)], mrecv.at[0])
            wait(ML.at[ms(0)], msend.at[0])
            MS[ms(1), :] = MS[ms(0), :] + ML[ms(0), :]
        else:
            n = 3 * stage - 3
            for d in (1, 2, 3):
                wait(ML.at[ms(n + d)], mrecv.at[n + d])
                wait(ML.at[ms(n + d)], msend.at[n + d])
            MS[ms(stage + 1), :] = (MS[ms(stage), :] + ML[ms(n + 2), :]) + (ML[ms(n + 1), :] + ML[ms(n + 3), :])

    def small0():
        small_send(0)

    def small4():
        small_take(3)
        store = pltpu.make_async_copy(MS.at[ms(4)], dsum_ref, mloc.at[0])
        store.start()
        store.wait()

    def small_mid(n):
        small_take(n - 1)
        small_send(n)

    small = [small0] + [functools.partial(small_mid, n) for n in (1, 2, 3)] + [small4]

    def rows_of(slot, c, n):
        return pl.ds(mo(slot * BATCH + c * n, n), n)

    def weight_load(q):
        l = jnp.where(q <= 7, q, 14 - q)
        return pltpu.make_async_copy(w_ref.at[l], WB.at[pl.ds(mo(lax.rem(q, 2) * W, W), W)], wsem.at[lax.rem(q, 2)])

    def weights(q):
        weight_load(q).wait()

        @pl.when(q < 13)
        def _():
            weight_load(q + 1).start()
        return pl.ds(mo(lax.rem(q, 2) * W, W), W)

    def forward(l):
        here = weights(l)

        def chunk(c, carry):
            h = rows_of(HIDDEN, c, FWD)
            z = jnp.dot(ACT[h, :], WB[here, :], preferred_element_type=F32).astype(BF16)
            ACT[rows_of(l, c, FWD), :] = z
            zf = z.astype(F32)
            t = jnp.tanh(GELU_SCALE * (zf + GELU_CUBIC * zf * zf * zf))
            ACT[h, :] = (0.5 * zf * (1.0 + t)).astype(BF16)
            return carry
        lax.fori_loop(0, BATCH // FWD, chunk, 0)

    def backward(l):
        here = weights(14 - l)

        def chunk(c, carry):
            dh = lax.dot_general(ACT[rows_of(l, c, BWD), :], WB[here, :], (((1,), (1,)), ((), ())), preferred_element_type=F32).astype(BF16)
            below = rows_of(l - 1, c, BWD)
            zf = ACT[below, :].astype(F32)
            t = jnp.tanh(GELU_SCALE * (zf + GELU_CUBIC * zf * zf * zf))
            ACT[rows_of(HIDDEN, c, BWD), :] = (0.5 * zf * (1.0 + t)).astype(BF16)
            slope = 0.5 * (1.0 + t) + 0.5 * zf * (1.0 - t * t) * GELU_SCALE * (1.0 + 3.0 * GELU_CUBIC * zf * zf)
            ACT[below, :] = (dh.astype(F32) * slope).astype(BF16)
            return carry
        lax.fori_loop(0, BATCH // BWD, chunk, 0)

    def gram(left, right, dst, lower, diag_row):
        val = lax.dot_general(ACT[rows_of(left, 0, BATCH), :], ACT[rows_of(right, 0, BATCH), :],
                              (((0,), (0,)), ((), ())), preferred_element_type=F32)
        out = pl.ds(dst, W)

        @pl.when(jnp.logical_not(lower))
        def _():
            Y[out, :] = val

        @pl.when(lower)
        def _():
            r = lax.broadcasted_iota(jnp.int32, (W, W), 0)
            q = lax.broadcasted_iota(jnp.int32, (W, W), 1)
            Y[out, :] = jnp.where(r > q, val, Y[out, :])
            MS[pl.ds(diag_row, 1), :] = jnp.sum(jnp.where(r == q, val, 0.0), axis=0, keepdims=True)

    tok_load = pltpu.make_async_copy(tok_ref, ACT.at[pl.ds(HIDDEN * BATCH, BATCH)], tsem.at[0])
    dout_load = pltpu.make_async_copy(dout_ref, ACT.at[pl.ds(7 * BATCH, BATCH)], tsem.at[1])

    def item(p, j):
        upd = is_update(p)
        is_a = p < 2
        pair = j // 2
        l_a = 4 * p + j
        l_g = 11 - 2 * p - j
        l_s = 30 - 4 * p - 2 * pair + lax.rem(j, 2)
        l = jnp.where(is_a, l_a, jnp.where(upd, l_g, l_s))

        @pl.when(is_a & (l > 0))
        def _():
            forward(l - 1)

        @pl.when(upd & (l > 0))
        def _():
            backward(l)

        @pl.when(upd & (l == 0))
        def _():
            tok_load.start()
            tok_load.wait()

        left = jnp.where(is_a | upd, HIDDEN, l)
        right = jnp.where(is_a, HIDDEN, l)
        which = jnp.where(upd, j, pair)
        diag_row = jnp.where(is_a, 2 * p, 2 * p - 8) + pair
        gram(left, right, produced(p, which), jnp.logical_not(upd) & (lax.rem(l, 2) == 1), jnp.where(upd, 0, diag_row))

    weight_load(0).start()
    tok_load.start()
    dout_load.start()
    load_inverses(2)
    tok_load.wait()
    dout_load.wait()

    def period(n_period, carry):
        t = n_period - 1
        for sub in range(3):
            for n in slots[sub]:
                p = t - n // 3

                @pl.when((p >= 0) & (p < ROUNDS))
                def _(n=n, p=p):
                    steps[n](p)
            for n in range(5):
                if n % 3 == sub:
                    pl.when(t == DIAG_PERIOD + n // 3)(small[n])

            @pl.when(t + 1 < ROUNDS)
            def _(sub=sub):
                if sub < 2:
                    item(t + 1, sub)
                else:
                    @pl.when(jnp.logical_not(is_update(t + 1)))
                    def _():
                        def more(j, carry):
                            item(t + 1, j)
                            return carry
                        lax.fori_loop(2, 4, more, 0)
        return carry

    lax.fori_loop(0, PERIODS + 1, period, 0)


def reduce_units(tok, dout, w, a_inv, s_inv):
    any_space = pl.BlockSpec(memory_space=pl.ANY)
    dma = pltpu.SemaphoreType.DMA
    return pl.pallas_call(
        comm_kernel,
        out_shape=(jax.ShapeDtypeStruct((8, W, W), F32), jax.ShapeDtypeStruct((8, W, W), F32), jax.ShapeDtypeStruct((8, W), F32)),
        in_specs=[any_space] * 5,
        out_specs=(any_space,) * 3,
        scratch_shapes=[
            pltpu.VMEM((NX * W, W), F32),
            pltpu.VMEM((NR * W, W), F32),
            pltpu.VMEM((NG * W, W), F32),
            pltpu.VMEM((2 * W, W), F32),
            pltpu.VMEM((4 * W, W), F32),
            pltpu.VMEM((9 * BATCH, W), BF16),
            pltpu.VMEM((2 * W, W), BF16),
            pltpu.VMEM((2 * W, W), F32),
            pltpu.VMEM((W, W), F32),
            pltpu.VMEM((40, W), F32),
            pltpu.VMEM((80, W), F32),
            dma((NR, 36)), dma((NR, 36)), *[dma((n,)) for n in (2, 2, 2, 2, 2, ROUNDS, 10, 10, 1, 2, 2)],
        ],
        compiler_params=pltpu.CompilerParams(collective_id=0, has_side_effects=True, vmem_limit_bytes=67043328),
        name='reduce_units',
    )(tok, dout, w, a_inv, s_inv)


def blend_kernel(p_ref, d_ref, a_ref, s_ref, u_ref, a_out, s_out, u_out):
    t, h = pl.program_id(0), pl.program_id(1)

    @pl.when(h == 0)
    def _():
        u_out[...] = u_ref[...]
    block = 128

    def write(old_ref, new_ref):
        for rb in range(W // block):
            rows = pl.ds(rb * block, block)
            here = p_ref[0, rows, :]
            turned = p_ref[0, :, rows].T
            r = lax.broadcasted_iota(jnp.int32, (block, W), 0) + rb * block
            c = lax.broadcasted_iota(jnp.int32, (block, W), 1)
            first = jnp.where(r <= c, here, turned)
            second = jnp.where(r == c, d_ref[pl.ds(t, 1), :], jnp.where(r < c, turned, here))
            value = jnp.where(h == 0, first, second) * SCALE
            new_ref[0, rows, :] = FACTOR_DECAY * old_ref[0, rows, :] + (1.0 - FACTOR_DECAY) * value
    pl.when(t < 4)(functools.partial(write, a_ref, a_out))
    pl.when(t >= 4)(functools.partial(write, s_ref, s_out))


def blend(packed, dsum, a_old, s_old, update):
    mat = functools.partial(pl.BlockSpec, (1, W, W))
    each = mat(lambda t, h: (t, 0, 0))
    a_spec = mat(lambda t, h: (jnp.where(t < 4, 2 * t + h, 7), 0, 0))
    s_spec = mat(lambda t, h: (jnp.where(t < 4, 6, 14 - 2 * t + h), 0, 0))
    shape = jax.ShapeDtypeStruct((8, W, W), F32)
    return pl.pallas_call(
        blend_kernel,
        grid=(8, 2),
        in_specs=[each, pl.BlockSpec((8, W), lambda t, h: (0, 0)), a_spec, s_spec, each],
        out_specs=(a_spec, s_spec, each),
        out_shape=(shape,) * 3,
        compiler_params=pltpu.CompilerParams(vmem_limit_bytes=60 * 1024 * 1024),
        name='blend',
    )(packed, dsum, a_old, s_old, update)


def solution(mesh):
    row_spec = P(('node', 'data'), None)
    full_spec = P()

    def per_device(tok, dout, w, a_prev, s_prev, a_pre, s_pre):
        packed, update, dsum = reduce_units(tok, dout, w, a_pre, s_pre)
        a_new, s_new, update = blend(packed, dsum, a_prev, s_prev, update)
        return update, a_new, s_new

    return jax.shard_map(per_device, mesh=mesh, in_specs=(row_spec, row_spec) + (full_spec,) * 5, out_specs=(full_spec,) * 3, check_vma=False)
```

profile of v0, /device:TPU:1, one launch (start us, length us, event | category | flops | bytes accessed | tf_op | source)
XLA Modules:
  0.0 284.3 jit_solution(17215981366870577262)
XLA Ops:
  0.6 231.4 %reduce_units.1 = (f32[8,768,768]{2,1,0:T(8,128)}, f32[8,768,768]{2,1,0:T(8,128)}, f32[8,768]{1,0:T(8,128)}) custom-call(bf16[1024,768]{1,0:T(8,128)(2,1)} %tok_ref.1, bf16[1024,768]{1,0:T(8,128)(2,1)} %dout_ref.1, bf16[8,768,768]{2,1,0:T(8,128)(2,1)} %w_ref.1, f32[8,768,768]{2,1,0:T(8,128)} %ainv_ref.1, f32[8,768,768]{2,1,0:T(8,128)} %sinv_ref.1), custom_call_target="tpu_custom_call" | custom-call | tf_op jit(solution)/shard_map/reduce_units/pallas_call | solution.py:477
  232.0 52.3 %blend.1 = (f32[8,768,768]{2,1,0:T(8,128)}, f32[8,768,768]{2,1,0:T(8,128)}, f32[8,768,768]{2,1,0:T(8,128)}) custom-call(f32[8,768,768]{2,1,0:T(8,128)} %get-tuple-element.9.p_ref, f32[8,768]{1,0:T(8,128)} %get-tuple-element.10.d_ref, f32[8,768,768]{2,1,0:T(8,128)} %a_ref.1, f32[8,768,768]{2,1,0:T(8,128)} %s_ref.1, f32[8,768,768]{2,1,0:T(8,128)} %get-tuple-element.11.u_ref), custom_call_target="tpu_custom_call" | custom-call | tf_op jit(solution)/shard_map/blend/pallas_call | solution.py:530
where the time goes:
time: 284 us
  Pallas kernels  284 us (100%)
    pallas_call x1, Pallas kernels, reduce_units(): pl.pallas_call(comm_kernel, out_shape=(jax.ShapeDtypeStruct((8, W, W), F3...  231 us
    pallas_call x1, Pallas kernels, blend(): pl.pallas_call(blend_kernel, grid=(8, 2), in_specs=[each, pl.BlockSpec((8...  52.3 us

commit v1 on v0

--- a/solution.py
+++ b/solution.py
@@ -23,6 +23,7 @@
 F32 = jnp.float32
 ALL = pl.ds(0, W)
 SCALE = 1.0 / 131072.0
+HALF = 384
 
 
 def comm_kernel(tok_ref, dout_ref, w_ref, ainv_ref, sinv_ref, packed_ref, upd_ref, dsum_ref,
@@ -197,12 +198,14 @@
     def step1(p):
         wait(dslot(p), drecv.at[lax.rem(p, 2)])
 
-        def some(c, carry):
-            a = pl.ds(mo(lax.rem(p, NX) * W + c * 64, 64), 64)
-            X[a, :] = Y[pl.ds(mo(produced(p, core) + c * 64, 64), 64), :] + D[pl.ds(mo(lax.rem(p, 2) * W + c * 64, 64), 64), :]
-            return carry
-        lax.fori_loop(0, 12, some, 0)
-        colours(scatter_a, p, 0)
+        for k in range(3):
+            def some(c, carry, k=k):
+                n = 256 * k + c * 64
+                X[pl.ds(mo(lax.rem(p, NX) * W + n, 64), 64), :] = (
+                    Y[pl.ds(mo(produced(p, core) + n, 64), 64), :] + D[pl.ds(mo(lax.rem(p, 2) * W + n, 64), 64), :])
+                return carry
+            lax.fori_loop(0, 4, some, 0)
+            scatter_a(p, k, 0)
 
     def step2(p):
         colours(scatter_b, p, 0)
@@ -420,6 +423,10 @@
         def _():
             forward(l - 1)
 
+        @pl.when(upd & (l == 7))
+        def _():
+            dout_load.wait()
+
         @pl.when(upd & (l > 0))
         def _():
             backward(l)
@@ -435,12 +442,11 @@
         diag_row = jnp.where(is_a, 2 * p, 2 * p - 8) + pair
         gram(left, right, produced(p, which), jnp.logical_not(upd) & (lax.rem(l, 2) == 1), jnp.where(upd, 0, diag_row))
 
+    tok_load.start()
     weight_load(0).start()
-    tok_load.start()
+    tok_load.wait()
     dout_load.start()
     load_inverses(2)
-    tok_load.wait()
-    dout_load.wait()
 
     def period(n_period, carry):
         t = n_period - 1
@@ -457,15 +463,18 @@
 
             @pl.when(t + 1 < ROUNDS)
             def _(sub=sub):
-                if sub < 2:
-                    item(t + 1, sub)
+                upd = is_update(t + 1)
+                if sub == 0:
+                    @pl.when(jnp.logical_not(upd))
+                    def _():
+                        item(t + 1, 0)
+                elif sub == 1:
+                    item(t + 1, jnp.where(upd, 0, 1))
                 else:
-                    @pl.when(jnp.logical_not(is_update(t + 1)))
-                    def _():
-                        def more(j, carry):
-                            item(t + 1, j)
-                            return carry
-                        lax.fori_loop(2, 4, more, 0)
+                    def more(j, carry):
+                        item(t + 1, j)
+                        return carry
+                    lax.fori_loop(jnp.where(upd, 1, 2), jnp.where(upd, 2, 4), more, 0)
         return carry
 
     lax.fori_loop(0, PERIODS + 1, period, 0)
@@ -500,38 +509,37 @@
 
 def blend_kernel(p_ref, d_ref, a_ref, s_ref, u_ref, a_out, s_out, u_out):
     t, h = pl.program_id(0), pl.program_id(1)
-
-    @pl.when(h == 0)
-    def _():
-        u_out[...] = u_ref[...]
+    u_out[...] = u_ref[...]
     block = 128
 
     def write(old_ref, new_ref):
-        for rb in range(W // block):
+        for rb in range(HALF // block):
             rows = pl.ds(rb * block, block)
-            here = p_ref[0, rows, :]
-            turned = p_ref[0, :, rows].T
-            r = lax.broadcasted_iota(jnp.int32, (block, W), 0) + rb * block
+            top = h * HALF + rb * block
+            far = pl.ds(pl.multiple_of(top, block), block)
+            here = p_ref[0, far, :]
+            turned = p_ref[0, :, far].T
+            r = lax.broadcasted_iota(jnp.int32, (block, W), 0) + top
             c = lax.broadcasted_iota(jnp.int32, (block, W), 1)
-            first = jnp.where(r <= c, here, turned)
-            second = jnp.where(r == c, d_ref[pl.ds(t, 1), :], jnp.where(r < c, turned, here))
-            value = jnp.where(h == 0, first, second) * SCALE
-            new_ref[0, rows, :] = FACTOR_DECAY * old_ref[0, rows, :] + (1.0 - FACTOR_DECAY) * value
+            first = jnp.where(r <= c, here, turned) * SCALE
+            second = jnp.where(r == c, d_ref[pl.ds(t, 1), :], jnp.where(r < c, turned, here)) * SCALE
+            new_ref[0, rows, :] = FACTOR_DECAY * old_ref[0, rows, :] + (1.0 - FACTOR_DECAY) * first
+            new_ref[1, rows, :] = FACTOR_DECAY * old_ref[1, rows, :] + (1.0 - FACTOR_DECAY) * second
     pl.when(t < 4)(functools.partial(write, a_ref, a_out))
     pl.when(t >= 4)(functools.partial(write, s_ref, s_out))
 
 
 def blend(packed, dsum, a_old, s_old, update):
-    mat = functools.partial(pl.BlockSpec, (1, W, W))
-    each = mat(lambda t, h: (t, 0, 0))
-    a_spec = mat(lambda t, h: (jnp.where(t < 4, 2 * t + h, 7), 0, 0))
-    s_spec = mat(lambda t, h: (jnp.where(t < 4, 6, 14 - 2 * t + h), 0, 0))
+    two = functools.partial(pl.BlockSpec, (2, HALF, W))
+    u_spec = pl.BlockSpec((1, HALF, W), lambda t, h: (t, h, 0))
+    a_spec = two(lambda t, h: (jnp.minimum(t, 3), jnp.where(t < 4, h, 1), 0))
+    s_spec = two(lambda t, h: (jnp.minimum(7 - t, 3), jnp.where(t < 4, 0, h), 0))
     shape = jax.ShapeDtypeStruct((8, W, W), F32)
     return pl.pallas_call(
         blend_kernel,
         grid=(8, 2),
-        in_specs=[each, pl.BlockSpec((8, W), lambda t, h: (0, 0)), a_spec, s_spec, each],
-        out_specs=(a_spec, s_spec, each),
+        in_specs=[pl.BlockSpec((1, W, W), lambda t, h: (t, 0, 0)), pl.BlockSpec((8, W), lambda t, h: (0, 0)), a_spec, s_spec, u_spec],
+        out_specs=(a_spec, s_spec, u_spec),
         out_shape=(shape,) * 3,
         compiler_params=pltpu.CompilerParams(vmem_limit_bytes=60 * 1024 * 1024),
         name='blend',

time: 284 us -> 277 us (0.975)
  Pallas kernels: 284 us -> 276 us
    pallas_call x1, Pallas kernels: 231 us -> 227 us  [reduce_units(): pl.pallas_call(comm_kernel, out_shape=(jax.ShapeDtypeStruct((8, W, W), F3...]
    pallas_call x1, Pallas kernels: 52.3 us -> 48.7 us  [blend(): pl.pallas_call(blend_kernel, grid=(8, 2), in_specs=[pl.BlockSpec((1, W, W...]
where the time goes in v1:
time: 277 us; the launch traced here: 276 us
  Pallas kernels  276 us (100%)
    pallas_call x1, Pallas kernels, reduce_units(): pl.pallas_call(comm_kernel, out_shape=(jax.ShapeDtypeStruct((8, W, W), F3...  227 us
    pallas_call x1, Pallas kernels, blend(): pl.pallas_call(blend_kernel, grid=(8, 2), in_specs=[pl.BlockSpec((1, W, W...  48.7 us

profile of v1, /device:TPU:1, one launch (start us, length us, event | category | flops | bytes accessed | tf_op | source)
XLA Modules:
  0.0 276.5 jit_solution(5709544062466122677)
XLA Ops:
  0.6 227.1 %reduce_units.1 = (f32[8,768,768]{2,1,0:T(8,128)}, f32[8,768,768]{2,1,0:T(8,128)}, f32[8,768]{1,0:T(8,128)}) custom-call(bf16[1024,768]{1,0:T(8,128)(2,1)} %tok_ref.1, bf16[1024,768]{1,0:T(8,128)(2,1)} %dout_ref.1, bf16[8,768,768]{2,1,0:T(8,128)(2,1)} %w_ref.1, f32[8,768,768]{2,1,0:T(8,128)} %ainv_ref.1, f32[8,768,768]{2,1,0:T(8,128)} %sinv_ref.1), custom_call_target="tpu_custom_call" | custom-call | tf_op jit(solution)/shard_map/reduce_units/pallas_call | solution.py:486
  227.7 48.7 %blend.1 = (f32[8,768,768]{2,1,0:T(8,128)}, f32[8,768,768]{2,1,0:T(8,128)}, f32[8,768,768]{2,1,0:T(8,128)}) custom-call(f32[8,768,768]{2,1,0:T(8,128)} %get-tuple-element.9.p_ref, f32[8,768]{1,0:T(8,128)} %get-tuple-element.10.d_ref, f32[8,768,768]{2,1,0:T(8,128)} %a_ref.1, f32[8,768,768]{2,1,0:T(8,128)} %s_ref.1, f32[8,768,768]{2,1,0:T(8,128)} %get-tuple-element.11.u_ref), custom_call_target="tpu_custom_call" | custom-call | tf_op jit(solution)/shard_map/blend/pallas_call | solution.py:538

commit v2 on v1

--- a/solution.py
+++ b/solution.py
@@ -131,6 +131,11 @@
         i, plus, minus = neighbours(k, s)
         jp, jm, j2 = around(i)
         fwd, blk, sa = rs(p, k, s, 0), rs(p, k, s, 1), ss(p, k, s, 0)
+        if s == 2:
+            send(X.at[region(p, k, s, jp)], R.at[landing(p, k, s, 1, 1)], sa, blk, plus)
+            send(X.at[region(p, k, s, jm)], R.at[landing(p, k, s, 1, 0)], sa, blk, minus)
+            send(X.at[region(p, k, s, j2)], R.at[landing(p, k, s, 0)], ss(p, k, s, 1), fwd, device((k + s) % 3, 2))
+            return
         send(X.at[region(p, k, s, j2, 0)], R.at[landing(p, k, s, 0, 0)], sa, fwd, minus)
         send(X.at[region(p, k, s, j2, 1)], R.at[landing(p, k, s, 0, 1)], sa, fwd, plus)
         send(X.at[region(p, k, s, jm, 1)], R.at[landing(p, k, s, 1, 0, 1)], sa, blk, minus)
@@ -154,6 +159,8 @@
         if s < 2:
             X[mine] = value
         else:
+            wait(R.at[landing(p, k, s, 0)], rs(p, k, s, 0))
+            value = value + R[landing(p, k, s, 0)]
             G[region(p, k, s, i, slots=NG)] = value
 
     def gather_a(p, k, s):
@@ -161,6 +168,8 @@
         mine = G.at[region(p, k, s, i, slots=NG)]
         send(mine, mine, ss(p, k, s, 2), rs(p, k, s, 2), plus)
         send(mine, mine, ss(p, k, s, 2), rs(p, k, s, 2), minus)
+        if s == 2:
+            send(mine, mine, ss(p, k, s, 3), rs(p, k, s, 3), device((k + s) % 3, 2))
 
     def gather_b(p, k, s):
         i, plus, minus = neighbours(k, s)
@@ -171,6 +180,8 @@
         send(from_plus, from_plus, ss(p, k, s, 3), rs(p, k, s, 3), minus)
 
     def gather_c(p, k, s):
+        if s == 2:
+            wait(R.at[landing(p, k, s, 1)], rs(p, k, s, 2))
         wait(R.at[landing(p, k, s, 0)], rs(p, k, s, 3))
 
     def colours(f, p, s):
@@ -223,9 +234,6 @@
         colours(scatter_a, p, 2)
 
     def step6(p):
-        colours(scatter_b, p, 2)
-
-    def step7(p):
         colours(scatter_c, p, 2)
         colours(gather_a, p, 2)
 
@@ -235,11 +243,7 @@
                 wait(R.at[landing(p, k, s, 1)], ss(p, k, s, w))
                 wait(R.at[landing(p, k, s, 0)], ss(p, k, s, w + 1))
 
-    def step8(p):
-        colours(gather_b, p, 2)
-        sent(p, 0)
-
-    def step9(p):
+    def step7(p):
         colours(gather_c, p, 2)
         colours(gather_a, p, 1)
 
@@ -251,14 +255,15 @@
         pltpu.make_async_copy(ainv_ref.at[l], inverse(0), isem.at[0]).start()
         pltpu.make_async_copy(sinv_ref.at[l], inverse(1), isem.at[1]).start()
 
-    def step10(p):
+    def step8(p):
         colours(gather_b, p, 1)
-
-    def step11(p):
+        sent(p, 0)
+
+    def step9(p):
         colours(gather_c, p, 1)
         colours(gather_a, p, 0)
 
-    def step12(p):
+    def step10(p):
         colours(gather_b, p, 0)
 
     def piece(p, part):
@@ -275,7 +280,7 @@
             pltpu.make_async_copy(UPD.at[here], out, osem.at[lax.rem(p, 2)]).start()
             send(UPD.at[here], out, osend.at[lax.rem(p, 2)], orecv.at[p], partner)
 
-    def step13(p):
+    def step11(p):
         colours(gather_c, p, 0)
 
         @pl.when(is_update(p))
@@ -290,26 +295,26 @@
             send(gslot(p), out, osend.at[lax.rem(p, 2)], orecv.at[p], partner)
         piece(p, 0)
 
-    def step14(p):
+    def step12(p):
         sent(p, 2)
         piece(p, 1)
 
-    def step15(p):
+    def step13(p):
         piece(p, 2)
 
         @pl.when(is_update(p) & is_update(p + 1))
         def _():
             load_inverses(p + 1)
 
-    def step16(p):
+    def step14(p):
         wait(xslot(p), osem.at[lax.rem(p, 2)])
         wait(xslot(p), osend.at[lax.rem(p, 2)])
 
-    def step17(p):
+    def step15(p):
         wait(xslot(p), orecv.at[p])
 
-    steps = [step0, step1, step2, step3, step4, step5, step6, step7, step8, step9, step10, step11, step12, step13, step14, step15, step16, step17]
-    slots = [(0, 6, 9, 12, 3, 15), (7, 10, 4, 1, 16, 13), (8, 5, 11, 2, 14, 17)]
+    steps = [step0, step1, step2, step3, step4, step5, step6, step7, step8, step9, step10, step11, step12, step13, step14, step15]
+    slots = [(0, 6, 9, 3, 12, 15), (7, 4, 1, 10, 13), (8, 5, 2, 14, 11)]
 
     def ms(n):
         return pl.ds(8 * n, 8)
@@ -469,12 +474,12 @@
                     def _():
                         item(t + 1, 0)
                 elif sub == 1:
-                    item(t + 1, jnp.where(upd, 0, 1))
-                else:
                     def more(j, carry):
                         item(t + 1, j)
                         return carry
-                    lax.fori_loop(jnp.where(upd, 1, 2), jnp.where(upd, 2, 4), more, 0)
+                    lax.fori_loop(jnp.where(upd, 0, 1), jnp.where(upd, 1, 3), more, 0)
+                else:
+                    item(t + 1, jnp.where(upd, 1, 3))
         return carry
 
     lax.fori_loop(0, PERIODS + 1, period, 0)

time: 277 us -> 275 us (level)
  no operation moved by 1% of the time
where the time goes in v2:
time: 275 us
  Pallas kernels  275 us (100%)
    pallas_call x1, Pallas kernels, reduce_units(): pl.pallas_call(comm_kernel, out_shape=(jax.ShapeDtypeStruct((8, W, W), F3...  226 us
    pallas_call x1, Pallas kernels, blend(): pl.pallas_call(blend_kernel, grid=(8, 2), in_specs=[pl.BlockSpec((1, W, W...  48.7 us

profile of v2, /device:TPU:1, one launch (start us, length us, event | category | flops | bytes accessed | tf_op | source)
XLA Modules:
  0.0 275.2 jit_solution(12930526216815020411)
XLA Ops:
  0.6 225.8 %reduce_units.1 = (f32[8,768,768]{2,1,0:T(8,128)}, f32[8,768,768]{2,1,0:T(8,128)}, f32[8,768]{1,0:T(8,128)}) custom-call(bf16[1024,768]{1,0:T(8,128)(2,1)} %tok_ref.1, bf16[1024,768]{1,0:T(8,128)(2,1)} %dout_ref.1, bf16[8,768,768]{2,1,0:T(8,128)(2,1)} %w_ref.1, f32[8,768,768]{2,1,0:T(8,128)} %ainv_ref.1, f32[8,768,768]{2,1,0:T(8,128)} %sinv_ref.1), custom_call_target="tpu_custom_call" | custom-call | tf_op jit(solution)/shard_map/reduce_units/pallas_call | solution.py:491
  226.5 48.7 %blend.1 = (f32[8,768,768]{2,1,0:T(8,128)}, f32[8,768,768]{2,1,0:T(8,128)}, f32[8,768,768]{2,1,0:T(8,128)}) custom-call(f32[8,768,768]{2,1,0:T(8,128)} %get-tuple-element.9.p_ref, f32[8,768]{1,0:T(8,128)} %get-tuple-element.10.d_ref, f32[8,768,768]{2,1,0:T(8,128)} %a_ref.1, f32[8,768,768]{2,1,0:T(8,128)} %s_ref.1, f32[8,768,768]{2,1,0:T(8,128)} %get-tuple-element.11.u_ref), custom_call_target="tpu_custom_call" | custom-call | tf_op jit(solution)/shard_map/blend/pallas_call | solution.py:543
